TPU v7x, 256 devices: a whole 4x4x8 slice. The times are simulated.
256 devices in a mesh: seq: 16 (over y, x), width: 16 (over z, core).
Axes of the slice: x: 4, y: 4, z: 8, core: 2. Of those that a mesh axis runs over, the one named last changes fastest.
Arguments:
- leak_rate: float32 [1, 32768, 2048], P(None, 'seq', 'width'), may hold values from 0.2 to 2
- signal_in: bfloat16 [1, 32768, 2048], P(None, 'seq', 'width'), may hold values from -6 to 6
- norm_gain: float32 [2048], P('width'), may hold values from 0.25 to 1.75
Outputs:
- mixed_out: bfloat16 [1, 32768, 2048], P(None, 'seq', 'width')
All inputs are finite; a program needn't handle non-finite values.
Results may differ from a plain program's by a relative error of at most 0.001.
Values sent between devices are 32-bit elements; how exact they have to be, the bound alone decides.
A program may use at most 64 MiB of HBM per device.

v0:
```python
import jax
import jax.numpy as jnp
from jax import lax
from jax.sharding import PartitionSpec as P


def copy_for_each(x, axis):
    length = lax.axis_size(axis)
    return lax.all_to_all(jnp.broadcast_to(x[None], (length, *x.shape)), axis, 0, 0, tiled=True)


def all_in_one(x, axis):
    leaves = jax.tree.leaves(x)
    turns = sorted(range(len(leaves)), key=lambda k: -leaves[k].size)
    width = (1, *leaves[turns[0]].shape)[-1]
    lines = [
        jnp.pad(leaves[k].reshape(-1), (0, -leaves[k].size % width)).reshape(-1, width)
        for k in turns
    ]
    both, at, found = (copy_for_each(jnp.concatenate(lines), axis), 0, {})
    for k, line in zip(turns, lines):
        section = both[:, at : at + len(line)].reshape(len(both), -1)
        found[k] = section[:, : leaves[k].size].reshape(-1, *leaves[k].shape)
        at += len(line)
    numbers = iter(range(len(leaves)))
    return jax.tree.map(lambda _: found[next(numbers)], x)


def joined_by_halves(pieces, combine):
    while len(jax.tree.leaves(pieces)[0]) > 1:
        pieces = jax.vmap(combine)(
            *(jax.tree.map(lambda part: part[side::2], pieces) for side in (0, 1))
        )
    return jax.tree.map(lambda part: part[0], pieces)


def carried_in(x, axis, combine, identity, reverse):
    length, here = (lax.axis_size(axis), lax.axis_index(axis))
    passed = jnp.arange(length) > here if reverse else jnp.arange(length) < here

    def kept(part, zero, own):
        part = jnp.where(
            passed.reshape(-1, *(1 for _ in own.shape)), part, jnp.asarray(zero, own.dtype)
        )
        return part[::-1] if reverse else part

    pieces = all_in_one(x, axis)
    return joined_by_halves(jax.tree.map(kept, pieces, identity, x), combine)


def taken_together(x, axis):
    everything = copy_for_each(x, axis)
    return jnp.sum(everything, axis=0)


def join_pair(earlier, later):
    return (earlier[0] * later[0], later[0] * earlier[1] + later[1])


def per_device(leak_rate, signal_in, norm_gain):
    total_length = leak_rate.shape[1] * lax.axis_size("seq")
    keep = jnp.exp(-leak_rate / total_length)
    push = signal_in.astype(jnp.float32) * total_length ** (-0.5)
    product, forward = lax.associative_scan(join_pair, (keep, push), axis=1)
    entering_forward = carried_in(
        (product[:, -1], forward[:, -1]),
        "seq",
        join_pair,
        (jnp.ones_like(keep[:, 0]), jnp.zeros_like(push[:, 0])),
        False,
    )
    forward = forward + product * entering_forward[1][:, None]
    product, backward = lax.associative_scan(join_pair, (keep, push), axis=1, reverse=True)
    entering_backward = carried_in(
        (product[:, 0], backward[:, 0]),
        "seq",
        join_pair,
        (jnp.ones_like(keep[:, 0]), jnp.zeros_like(push[:, 0])),
        True,
    )
    backward = backward + product * entering_backward[1][:, None]
    states = forward + backward
    power = taken_together(jnp.sum(states * states, axis=-1, keepdims=True), "width") / (
        states.shape[-1] * lax.axis_size("width")
    )
    mixed_out = (states * lax.rsqrt(power + 1e-06) * norm_gain).astype(jnp.bfloat16)
    return mixed_out


def solution(mesh):
    return jax.shard_map(
        per_device,
        mesh=mesh,
        in_specs=(P(None, "seq", "width"), P(None, "seq", "width"), P("width")),
        out_specs=P(None, "seq", "width"),
        check_vma=False,
    )
```

profile of v0, /device:TPU:1, one launch (start us, length us, event | category | flops | bytes accessed | tf_op | source)
XLA Modules:
  0.0 174.3 jit_solution(18346466432469344434)
XLA Ops:
  0.0 1.4 multiply_exponential_fusion
  1.4 0.7 slice.786
  2.1 0.7 slice.782
  2.8 2.1 %slice.904 = f32[1,1023,128]{2,1,0:T(8,128)} slice(f32[1,2048,128]{2,1,0:T(8,128)S(1)} %multiply_exponential_fusion), slice={[0:1:1], [1:2046:2], [0:128:1]} | slice | bytes 1047552 | tf_op jit(solution)/shard_map/slice | solution.py:73
  4.9 5.2 %reverse.13 = f32[1,2048,128]{2,1,0:T(8,128)} reverse(bf16[1,2048,128]{2,1,0:T(8,128)(2,1)S(1)} %copy-done.9), dimensions={1} | reverse | bytes 1572864 | tf_op jit(solution)/shard_map/reverse
  10.1 1.3 broadcast_multiply_fusion
  11.4 2.1 %slice.986 = f32[1,1023,128]{2,1,0:T(8,128)} slice(f32[1,2048,128]{2,1,0:T(8,128)S(1)} %broadcast_multiply_fusion), slice={[0:1:1], [2:2048:2], [0:128:1]} | slice | bytes 1047552 | tf_op jit(solution)/shard_map/slice | solution.py:73
  13.4 2.0 %slice.908 = f32[1,1024,128]{2,1,0:T(8,128)} slice(f32[1,2048,128]{2,1,0:T(8,128)S(1)} %broadcast_multiply_fusion), slice={[0:1:1], [1:2048:2], [0:128:1]} | slice | bytes 1048576 | tf_op jit(solution)/shard_map/slice | solution.py:73
  15.5 2.0 %slice.907 = f32[1,1024,128]{2,1,0:T(8,128)} slice(f32[1,2048,128]{2,1,0:T(8,128)S(1)} %broadcast_multiply_fusion), slice={[0:1:1], [0:2047:2], [0:128:1]} | slice | bytes 1048576 | tf_op jit(solution)/shard_map/slice | solution.py:73
  17.5 2.6 %slice.910 = f32[1,1024,128]{2,1,0:T(8,128)} reverse(f32[1,1024,128]{2,1,0:T(8,128)S(1)} %slice.782), dimensions={1} | reverse | bytes 1048576 | tf_op jit(solution)/shard_map/slice | solution.py:73
  20.1 2.6 %slice.906 = f32[1,1024,128]{2,1,0:T(8,128)} reverse(f32[1,1024,128]{2,1,0:T(8,128)S(1)} %slice.786), dimensions={1} | reverse | bytes 1048576 | tf_op jit(solution)/shard_map/slice | solution.py:73
  22.7 1.6 fusion.18
  24.7 1.4 slice.912
  26.1 1.3 slice.911
  27.4 1.4 slice.984
  29.2 1.4 slice.913
  30.6 1.0 fusion.20
  33.9 2.7 %slice.905 = f32[1,1023,128]{2,1,0:T(8,128)} reverse(f32[1,1023,128]{2,1,0:T(8,128)S(1)} %copy-done.11), dimensions={1} | reverse | bytes 1047552 | tf_op jit(solution)/shard_map/slice | solution.py:73
  37.8 0.7 add.566
  38.9 0.8 add_multiply_fusion.4
  39.8 0.9 copy-done.18
  40.7 0.7 pad_maximum_fusion.7
  41.4 1.0 pad.352
  42.5 2.6 %pad.353 = f32[1,1024,128]{2,1,0:T(8,128)} pad(f32[1,512,128]{2,1,0:T(8,128)} %add.566, f32[]{:T(128)} %constant.5.clone.1), padding=0_0_0x1_0_1x0_0_0 | pad | bytes 786436 | tf_op jit(solution)/shard_map/pad | solution.py:73
  45.1 1.7 pad.331
  46.7 2.0 %add.555 = f32[1,1024,128]{2,1,0:T(8,128)} add(f32[1,1024,128]{2,1,0:T(8,128)S(1)} %pad.330, f32[1,1024,128]{2,1,0:T(8,128)} %pad.331) | non-fusion elementwise | flops 131072 | bytes 1572864 | tf_op jit(solution)/shard_map/add | solution.py:73
  48.7 0.9 add.567
  50.2 1.0 add_multiply_fusion
  51.2 0.9 pad_maximum_fusion.2
  52.1 2.1 %pad.332 = f32[1,2048,128]{2,1,0:T(8,128)S(1)} pad(f32[1,1024,128]{2,1,0:T(8,128)} %pad_maximum_fusion.2, f32[]{:T(128)} %constant.5.clone.1), padding=0_0_0x0_1_1x0_0_0 | pad | bytes 1572868 | tf_op jit(solution)/shard_map/pad | solution.py:73
  54.2 1.9 %pad_maximum_fusion.3 = f32[1,1024,128]{2,1,0:T(8,128)} fusion(f32[1,1023,128]{2,1,0:T(8,128)} %get-tuple-element.13, f32[1,1,128]{2,1,0:T(1,128)S(1)} %get-tuple-element.8), kind=kLoop, calls=%fused_computation.13 | loop fusion | flops 131072 | bytes 1048576 | tf_op jit(solution)/shard_map/concatenate | solution.py:73
  56.1 4.6 %pad.354 = f32[1,2048,128]{2,1,0:T(8,128)} pad(f32[1,1024,128]{2,1,0:T(8,128)} %pad_maximum_fusion.3, f32[]{:T(128)} %constant.5.clone.1), padding=0_0_0x0_1_1x0_0_0 | pad | bytes 1572868 | tf_op jit(solution)/shard_map/pad | solution.py:73
  60.7 4.6 %pad.355 = f32[1,2048,128]{2,1,0:T(8,128)} pad(f32[1,1024,128]{2,1,0:T(8,128)} %add.567, f32[]{:T(128)} %constant.5.clone.1), padding=0_0_0x1_0_1x0_0_0 | pad | bytes 1572868 | tf_op jit(solution)/shard_map/pad | solution.py:73
  65.3 4.6 %pad.333 = f32[1,2048,128]{2,1,0:T(8,128)} pad(f32[1,1024,128]{2,1,0:T(8,128)} %add.555, f32[]{:T(128)} %constant.5.clone.1), padding=0_0_0x1_0_1x0_0_0 | pad | bytes 1572868 | tf_op jit(solution)/shard_map/pad | solution.py:73
  69.8 0.7 add_bitcast_fusion.1
  70.5 0.7 add_bitcast_fusion
  71.8 7.6 %all-to-all-start.1 = ((f32[16,2,128]{2,1,0:T(2,128)}), f32[16,2,128]{2,1,0:T(2,128)S(1)}, u32[]{:S(2)}, u32[]{:S(2)}) async-start(f32[16,2,128]{2,1,0:T(2,128)} %broadcast_in_dim.51), calls=%async_computation.1 | async-start | bytes 32768 | tf_op jit(solution)/shard_map/all_to_all | solution.py:9
  79.4 2.1 %slice.781 = f32[1,1023,128]{2,1,0:T(8,128)} slice(f32[1,2048,128]{2,1,0:T(8,128)S(1)} %multiply_exponential_fusion), slice={[0:1:1], [2:2048:2], [0:128:1]} | slice | bytes 1047552 | tf_op jit(solution)/shard_map/slice | solution.py:64
  81.5 1.1 broadcast_multiply_fusion.1
  82.6 2.1 %slice.862 = f32[1,1023,128]{2,1,0:T(8,128)} slice(f32[1,2048,128]{2,1,0:T(8,128)S(1)} %broadcast_multiply_fusion.1), slice={[0:1:1], [2:2048:2], [0:128:1]} | slice | bytes 1047552 | tf_op jit(solution)/shard_map/slice | solution.py:64
  84.7 2.1 %slice.784 = f32[1,1024,128]{2,1,0:T(8,128)} slice(f32[1,2048,128]{2,1,0:T(8,128)S(1)} %broadcast_multiply_fusion.1), slice={[0:1:1], [1:2048:2], [0:128:1]} | slice | bytes 1048576 | tf_op jit(solution)/shard_map/slice | solution.py:64
  86.8 2.0 %slice.783 = f32[1,1024,128]{2,1,0:T(8,128)} slice(f32[1,2048,128]{2,1,0:T(8,128)S(1)} %broadcast_multiply_fusion.1), slice={[0:1:1], [0:2047:2], [0:128:1]} | slice | bytes 1048576 | tf_op jit(solution)/shard_map/slice | solution.py:64
  88.8 1.3 fusion.17
  91.0 1.4 slice.787
  92.3 1.4 slice.860
  97.9 0.9 copy-done.19
  99.3 0.8 add.507
  100.1 0.9 add.519
  101.5 1.0 add_multiply_fusion.2
  102.5 2.7 %pad.288 = f32[1,2048,128]{2,1,0:T(8,128)} pad(f32[1,1024,128]{2,1,0:T(8,128)S(1)} %pad_maximum_fusion, f32[]{:T(128)} %constant.5.clone.1), padding=0_0_0x0_1_1x0_0_0 | pad | bytes 1572868 | tf_op jit(solution)/shard_map/pad | solution.py:64
  105.3 2.7 %pad.310 = f32[1,2048,128]{2,1,0:T(8,128)} pad(f32[1,1024,128]{2,1,0:T(8,128)S(1)} %pad_maximum_fusion.1, f32[]{:T(128)} %constant.5.clone.1), padding=0_0_0x0_1_1x0_0_0 | pad | bytes 1572868 | tf_op jit(solution)/shard_map/pad | solution.py:64
  108.0 2.7 %pad.311 = f32[1,2048,128]{2,1,0:T(8,128)} pad(f32[1,1024,128]{2,1,0:T(8,128)S(1)} %copy-done.10, f32[]{:T(128)} %constant.5.clone.1), padding=0_0_0x1_0_1x0_0_0 | pad | bytes 1572868 | tf_op jit(solution)/shard_map/pad | solution.py:64
  110.7 4.7 %pad.289 = f32[1,2048,128]{2,1,0:T(8,128)} pad(f32[1,1024,128]{2,1,0:T(8,128)} %add.507, f32[]{:T(128)} %constant.5.clone.1), padding=0_0_0x1_0_1x0_0_0 | pad | bytes 1572868 | tf_op jit(solution)/shard_map/pad | solution.py:64
  115.4 0.7 add_bitcast_fusion.3
  116.1 0.7 add_bitcast_fusion.2
  116.8 1.1 add.568
  118.4 1.1 add.557
  120.0 5.1 %rev.14 = f32[1,2048,128]{2,1,0:T(8,128)} reverse(f32[1,2048,128]{2,1,0:T(8,128)S(1)} %copy-done.8), dimensions={1} | reverse | bytes 2097152 | tf_op jit(solution)/shard_map/rev | solution.py:73
  125.2 9.0 %rev.13 = f32[1,2048,128]{2,1,0:T(8,128)} reverse(f32[1,2048,128]{2,1,0:T(8,128)} %add.557), dimensions={1} | reverse | bytes 2097152 | tf_op jit(solution)/shard_map/rev | solution.py:73
  134.8 6.6 %all-to-all-start = ((f32[16,2,128]{2,1,0:T(2,128)}), f32[16,2,128]{2,1,0:T(2,128)S(1)}, u32[]{:S(2)}, u32[]{:S(2)}) async-start(f32[16,2,128]{2,1,0:T(2,128)} %broadcast_in_dim.47), calls=%async_computation | async-start | bytes 32768 | tf_op jit(solution)/shard_map/all_to_all | solution.py:9
  141.5 6.3 %all-to-all-done = f32[16,2,128]{2,1,0:T(2,128)S(1)} async-done(((f32[16,2,128]{2,1,0:T(2,128)}), f32[16,2,128]{2,1,0:T(2,128)S(1)}, u32[]{:S(2)}, u32[]{:S(2)}) %all-to-all-start) | async-done | bytes 16416 | tf_op jit(solution)/shard_map/all_to_all | solution.py:9
  148.1 3.2 %multiply_reduce_fusion = (f32[2048]{0:T(1024)S(1)}, f32[1,2048,128]{2,1,0:T(8,128)}) fusion(f32[1,2048,128]{2,1,0:T(8,128)} %rev.13, f32[1,2048,128]{2,1,0:T(8,128)} %rev.14, f32[128]{0:T(128)S(1)} %fusion.14, f32[128]{0:T(128)S(1)} %fusion.15, f32[1,2048,128]{2,1,0:T(8,128)S(1)} %copy-done.6, f32[1,2048,128]{2,1,0:T(8,128)S(1)} %copy-done.7, ...), kind=kLoop, calls=%fused_computation.1 | loop fusion | flops 2357248 | bytes 7349248 | tf_op jit(solution)/shard_map/reduce_sum | solution.py:83
  151.3 19.8 %all_to_all.15 = f32[16,1,2048,1]{2,3,1,0:T(1,128)S(1)} all-to-all(f32[16,1,2048,1]{2,3,1,0:T(1,128)S(1)} %broadcast_in_dim.52), channel_id=1, replica_groups=mesh['seq'=16,'width'=16] {'width'}, dimensions={0} | all-to-all | bytes 262144 | tf_op jit(solution)/shard_map/all_to_all | solution.py:9
  171.9 2.4 %multiply_convert_fusion = bf16[1,2048,128]{2,1,0:T(8,128)(2,1)} fusion(f32[1,2048,128]{2,1,0:T(8,128)} %get-tuple-element.6, f32[128]{0:T(128)S(1)} %copy-done.23, f32[2048]{0:T(1024)S(1)} %add_rsqrt_fusion), kind=kLoop, calls=%fused_computation | loop fusion | flops 786432 | bytes 1581568 | tf_op jit(solution)/shard_map/convert_element_type | solution.py:86
  (376 shorter events, 13.2 us)
Async XLA Ops:
  2.8 2.1 %copy-start.9 = (bf16[1,2048,128]{2,1,0:T(8,128)(2,1)S(1)}, bf16[1,2048,128]{2,1,0:T(8,128)(2,1)}, u32[]{:S(2)}) copy-start(bf16[1,2048,128]{2,1,0:T(8,128)(2,1)} %param.4) | copy-start | bytes 1572868
  29.2 1.4 copy-start.17
  32.9 1.0 copy-start.11
  37.8 1.0 copy-start.21
  37.8 1.1 copy-start.22
  39.7 1.0 copy-start.18
  46.7 2.0 %copy-start = (f32[1,1024,128]{2,1,0:T(8,128)S(1)}, f32[1,1024,128]{2,1,0:T(8,128)}, u32[]{:S(2)}) copy-start(f32[1,1024,128]{2,1,0:T(8,128)} %pad.353) | copy-start | bytes 1572868
  48.7 1.2 copy-start.1
  48.7 1.4 copy-start.14
  48.7 1.5 copy-start.15
  71.8 62.3 %all-to-all-start.1 = ((f32[16,2,128]{2,1,0:T(2,128)}), f32[16,2,128]{2,1,0:T(2,128)S(1)}, u32[]{:S(2)}, u32[]{:S(2)}) async-start(f32[16,2,128]{2,1,0:T(2,128)} %broadcast_in_dim.51), calls=%async_computation.1 | async-start | bytes 32768 | tf_op jit(solution)/shard_map/all_to_all | solution.py:9
  97.8 1.0 copy-start.19
  97.8 1.0 copy-start.20
  100.1 1.2 copy-start.12
  100.1 1.4 copy-start.13
  102.5 2.7 %copy-start.16 = (f32[1,1023,128]{2,1,0:T(8,128)S(1)}, f32[1,1023,128]{2,1,0:T(8,128)}, u32[]{:S(2)}) copy-start(f32[1,1023,128]{2,1,0:T(8,128)} %get-tuple-element.9) | copy-start | bytes 1571332
  105.3 2.7 %copy-start.10 = (f32[1,1024,128]{2,1,0:T(8,128)S(1)}, f32[1,1024,128]{2,1,0:T(8,128)}, u32[]{:S(2)}) copy-start(f32[1,1024,128]{2,1,0:T(8,128)} %add.519) | copy-start | bytes 1572868
  108.0 8.8 %copy-start.4 = (f32[1,2048,128]{2,1,0:T(8,128)S(1)}, f32[1,2048,128]{2,1,0:T(8,128)}, u32[]{:S(2)}) copy-start(f32[1,2048,128]{2,1,0:T(8,128)} %pad.355) | copy-start | bytes 3145732
  110.7 6.1 %copy-start.2 = (f32[1,2048,128]{2,1,0:T(8,128)S(1)}, f32[1,2048,128]{2,1,0:T(8,128)}, u32[]{:S(2)}) copy-start(f32[1,2048,128]{2,1,0:T(8,128)} %pad.354) | copy-start | bytes 3145732
  116.8 1.6 copy-start.3
  118.4 1.6 copy-start.8
  120.0 28.1 %copy-start.7 = (f32[1,2048,128]{2,1,0:T(8,128)S(1)}, f32[1,2048,128]{2,1,0:T(8,128)}, u32[]{:S(2)}) copy-start(f32[1,2048,128]{2,1,0:T(8,128)} %pad.311) | copy-start | bytes 3145732
  125.2 22.9 %copy-start.5 = (f32[1,2048,128]{2,1,0:T(8,128)S(1)}, f32[1,2048,128]{2,1,0:T(8,128)}, u32[]{:S(2)}) copy-start(f32[1,2048,128]{2,1,0:T(8,128)} %pad.288) | copy-start | bytes 3145732
  125.2 22.9 %copy-start.6 = (f32[1,2048,128]{2,1,0:T(8,128)S(1)}, f32[1,2048,128]{2,1,0:T(8,128)}, u32[]{:S(2)}) copy-start(f32[1,2048,128]{2,1,0:T(8,128)} %pad.310) | copy-start | bytes 3145732
  134.8 13.1 %all-to-all-start = ((f32[16,2,128]{2,1,0:T(2,128)}), f32[16,2,128]{2,1,0:T(2,128)S(1)}, u32[]{:S(2)}, u32[]{:S(2)}) async-start(f32[16,2,128]{2,1,0:T(2,128)} %broadcast_in_dim.47), calls=%async_computation | async-start | bytes 32768 | tf_op jit(solution)/shard_map/all_to_all | solution.py:9
  171.3 0.7 copy-start.23
where the time goes:
time: 176 us; the launch traced here: 174 us
  local copies, waits for them, and re-layouts  100 us (57%)
  other arithmetic  31.5 us (18%)
  blocking collectives  19.8 us (11%)
  starting transfers between devices  14.2 us (8%)
  waiting for transfers between devices  6.32 us (4%)
  between operations  2.08 us (1%)
    slice x76, local copies, waits for them, and re-layouts, per_device(): lax.associative_scan(join_pair, (keep, push), axis=1, reverse=True)  23.8 us
    pad x40, local copies, waits for them, and re-layouts, per_device(): lax.associative_scan(join_pair, (keep, push), axis=1, reverse=True)  21.6 us
    all_to_all x1, blocking collectives, copy_for_each(): lax.all_to_all(jnp.broadcast_to(x[None], (length, *x.shape)), axis, 0, 0,...  19.8 us
    slice x76, local copies, waits for them, and re-layouts, per_device(): product, forward = lax.associative_scan(join_pair, (keep, push), axis=1)  15.6 us
    all_to_all x2, starting transfers between devices, copy_for_each(): lax.all_to_all(jnp.broadcast_to(x[None], (length, *x.shape)), axis, 0, 0,...  14.2 us
    rev x2, local copies, waits for them, and re-layouts, per_device(): lax.associative_scan(join_pair, (keep, push), axis=1, reverse=True)  14.1 us
    pad x40, local copies, waits for them, and re-layouts, per_device(): product, forward = lax.associative_scan(join_pair, (keep, push), axis=1)  13.4 us
    mul x44, other arithmetic, join_pair(): return (earlier[0] * later[0], later[0] * earlier[1] + later[1])  7.33 us
  transfers between devices with their start and end apart: 2, of which 1 were waited for; matrix products, arithmetic and copies ran while one was open for 29% of the time, Pallas kernels for 0%

commit v1 on v0

v1 whole, which is shorter than its diff:
```python
import functools

import jax
import jax.numpy as jnp
from jax import lax
from jax.experimental import pallas as pl
from jax.experimental.pallas import tpu as pltpu
from jax.sharding import PartitionSpec as P

MESH = pl.DeviceIdType.MESH
ROWS = 128
NT = (((1,), (1,)), ((), ()))


def ring_order(sizes):
    offsets = [()]
    for n in sizes:
        offsets = [o + (d,) for o in offsets for d in range(n)]
    far = lambda o: sum(min(d, n - d) for d, n in zip(o, sizes))
    return sorted((o for o in offsets if any(o)), key=lambda o: -far(o))


def split(x):
    high = x.astype(jnp.bfloat16)
    return high, (x - high.astype(jnp.float32)).astype(jnp.bfloat16)


def kernel(
    length, channels, seq_sizes, width_sizes,
    leak_hbm, signal_hbm, gain_ref, out_hbm,
    leak, signal, decay, grow, states, out,
    carried_f, decayed_f, carried_b, decayed_b,
    own_carry, got_carry, own_power, got_power,
    in_sem, out_sem, carry_send, carry_recv, power_send, power_recv,
):
    f32 = jnp.float32
    seq_n, width_n = seq_sizes[0] * seq_sizes[1], width_sizes[0] * width_sizes[1]
    seq, width = lax.axis_index("seq"), lax.axis_index("width")
    blocks = leak.shape[0] // ROWS

    def partner(here, sizes, offset):
        major = lax.rem(here // sizes[1] + offset[0], sizes[0])
        minor = lax.rem(lax.rem(here, sizes[1]) + offset[1], sizes[1])
        return major * sizes[1] + minor

    seq_partners = [partner(seq, seq_sizes, o) for o in ring_order(seq_sizes)]
    width_partners = [partner(width, width_sizes, o) for o in ring_order(width_sizes)]

    barrier = pltpu.get_barrier_semaphore()
    for other in seq_partners:
        pl.semaphore_signal(barrier, inc=1, device_id={"seq": other}, device_id_type=MESH)
    for other in width_partners:
        pl.semaphore_signal(barrier, inc=1, device_id={"width": other}, device_id_type=MESH)
    parts = in_sem.shape[1]
    part = leak.shape[0] // parts
    loads = []
    for k in range(parts):
        rows = pl.ds(k * part, part)
        loads.append((
            pltpu.make_async_copy(leak_hbm.at[rows], leak.at[rows], in_sem.at[0, k]),
            pltpu.make_async_copy(signal_hbm.at[rows], signal.at[rows], in_sem.at[1, k]),
        ))
        for load in loads[-1]:
            load.start()

    row = lax.broadcasted_iota(jnp.int32, (ROWS, ROWS), 0)
    col = lax.broadcasted_iota(jnp.int32, (ROWS, ROWS), 1)
    upto = jnp.where(col <= row, 1.0, 0.0).astype(jnp.bfloat16)
    upto = jnp.concatenate([upto, upto], axis=1)

    ends, sums_f, sums_b = [], [], []
    for pair in range(blocks // 2):
        if (pair * 2 * ROWS) % part == 0:
            for load in loads[pair * 2 * ROWS // part]:
                load.wait()
        two = [pl.ds((2 * pair + side) * ROWS, ROWS) for side in (0, 1)]
        steps = [leak[rows] * (1.0 / length) for rows in two]
        pieces = [split(step) for step in steps]
        summed = jnp.dot(
            upto,
            jnp.concatenate(
                [jnp.concatenate([p[k] for p in pieces], axis=1) for k in (0, 1)], axis=0
            ),
            preferred_element_type=f32,
        )
        for side in (0, 1):
            rows = two[side]
            through = summed[:, side * ROWS : (side + 1) * ROWS]
            before = through - steps[side]
            push = signal[rows]
            wide = push.astype(f32)
            extra_f = (wide * (jnp.exp(through) - 1.0)).astype(jnp.bfloat16)
            extra_b = (wide * (jnp.exp(-before) - 1.0)).astype(jnp.bfloat16)
            both = jnp.dot(
                upto,
                jnp.concatenate(
                    [
                        jnp.concatenate([push, push], axis=1),
                        jnp.concatenate([extra_f, extra_b], axis=1),
                    ],
                    axis=0,
                ),
                preferred_element_type=f32,
            )
            down, up = jnp.exp(-through), jnp.exp(before)
            sum_f, sum_b = both[:, :ROWS], both[:, ROWS:]
            decay[rows] = down
            grow[rows] = up
            states[rows] = down * sum_f + (wide - up * sum_b)
            ends.append(down[ROWS - 1 :])
            sums_f.append(down[ROWS - 1 :] * sum_f[ROWS - 1 :])
            sums_b.append(sum_b[ROWS - 1 :])

    at, product = jnp.zeros_like(ends[0]), jnp.ones_like(ends[0])
    for b in range(blocks):
        carried_f[b : b + 1] = at
        decayed_f[b : b + 1] = product
        at, product = at * ends[b] + sums_f[b], product * ends[b]
    own_carry[0:1] = product
    own_carry[1:2] = at
    at, product = jnp.zeros_like(ends[0]), jnp.ones_like(ends[0])
    for b in reversed(range(blocks)):
        at, product = at * ends[b] + sums_b[b], product * ends[b]
        carried_b[b : b + 1] = at
        decayed_b[b : b + 1] = product
    own_carry[2:3] = at
    got_carry[seq] = own_carry[...]

    pl.semaphore_wait(barrier, seq_n + width_n - 2)

    sends = []
    for k, other in enumerate(seq_partners):
        sends.append(pltpu.make_async_remote_copy(
            src_ref=own_carry, dst_ref=got_carry.at[seq],
            send_sem=carry_send.at[k], recv_sem=carry_recv.at[k],
            device_id={"seq": other}, device_id_type=MESH,
        ))
        sends[-1].start()
    for send in sends:
        send.wait_recv()

    into_f, into_b = jnp.zeros_like(ends[0]), jnp.zeros_like(ends[0])
    for j in range(seq_n):
        into_f = jnp.where(j < seq, into_f * got_carry[j, 0:1] + got_carry[j, 1:2], into_f)
        i = seq_n - 1 - j
        into_b = jnp.where(i > seq, into_b * got_carry[i, 0:1] + got_carry[i, 2:3], into_b)
    carried_f[...] = carried_f[...] + decayed_f[...] * into_f
    carried_b[...] = carried_b[...] + decayed_b[...] * into_b

    ones = jnp.ones((8, 2 * ROWS), jnp.bfloat16)
    for pair in range(blocks // 2):
        squares = []
        for b in (2 * pair, 2 * pair + 1):
            rows = pl.ds(b * ROWS, ROWS)
            value = (
                states[rows]
                + decay[rows] * carried_f[b : b + 1]
                + grow[rows] * carried_b[b : b + 1]
            )
            states[rows] = value
            squares.append(jnp.concatenate(split(value * value), axis=1))
        power = lax.dot_general(
            ones, jnp.concatenate(squares, axis=0), NT, preferred_element_type=f32
        )
        own_power[2 * pair : 2 * pair + 1] = power[0:1, :ROWS]
        own_power[2 * pair + 1 : 2 * pair + 2] = power[0:1, ROWS:]
    got_power[width] = own_power[...]

    for k, other in enumerate(width_partners):
        send = pltpu.make_async_remote_copy(
            src_ref=own_power, dst_ref=got_power.at[width],
            send_sem=power_send.at[k], recv_sem=power_recv.at[k],
            device_id={"width": other}, device_id_type=MESH,
        )
        send.start()
        sends.append(send)

    gain = gain_ref[...] * length**-0.5
    for b in range(blocks):
        rows = pl.ds(b * ROWS, ROWS)
        states[rows] = states[rows] * gain

    for send in sends[seq_n - 1 :]:
        send.wait_recv()
    total = got_power[0]
    for j in range(1, width_n):
        total = total + got_power[j]
    scale = lax.rsqrt(total * (1.0 / (channels * length)) + 1e-06)
    scale = jnp.concatenate([scale, jnp.zeros((ROWS - blocks, ROWS), f32)], axis=0).T

    parts = out_sem.shape[0]
    part = leak.shape[0] // parts
    stores = []
    for b in range(blocks):
        rows = pl.ds(b * ROWS, ROWS)
        out[rows] = (states[rows] * scale[:, b : b + 1]).astype(out.dtype)
        if (b + 1) * ROWS % part == 0:
            k = (b + 1) * ROWS // part - 1
            rows = pl.ds(k * part, part)
            stores.append(pltpu.make_async_copy(out.at[rows], out_hbm.at[rows], out_sem.at[k]))
            stores[-1].start()
    for send in sends:
        send.wait_send()
    for store in stores:
        store.wait()


def solution(mesh):
    sizes = dict(mesh.shape)
    seq_n, width_n = sizes["seq"], sizes["width"]
    seq_sizes, width_sizes = (4, seq_n // 4), (width_n // 2, 2)

    def per_device(leak_rate, signal_in, norm_gain):
        _, rows, lanes = leak_rate.shape
        length, channels = rows * seq_n, lanes * width_n
        blocks = rows // ROWS
        f32 = jnp.float32
        vmem, dma = pltpu.VMEM, pltpu.SemaphoreType.DMA
        out = pl.pallas_call(
            functools.partial(kernel, length, channels, seq_sizes, width_sizes),
            out_shape=jax.ShapeDtypeStruct((rows, lanes), jnp.bfloat16),
            in_specs=[
                pl.BlockSpec(memory_space=pl.ANY),
                pl.BlockSpec(memory_space=pl.ANY),
                pl.BlockSpec(memory_space=pltpu.VMEM),
            ],
            out_specs=pl.BlockSpec(memory_space=pl.ANY),
            scratch_shapes=[
                vmem((rows, lanes), f32),
                vmem((rows, lanes), jnp.bfloat16),
                vmem((rows, lanes), f32),
                vmem((rows, lanes), f32),
                vmem((rows, lanes), f32),
                vmem((rows, lanes), jnp.bfloat16),
                vmem((blocks, lanes), f32),
                vmem((blocks, lanes), f32),
                vmem((blocks, lanes), f32),
                vmem((blocks, lanes), f32),
                vmem((3, lanes), f32),
                vmem((seq_n, 3, lanes), f32),
                vmem((blocks, lanes), f32),
                vmem((width_n, blocks, lanes), f32),
                dma((2, 4)),
                dma((4,)),
                dma((seq_n - 1,)),
                dma((seq_n - 1,)),
                dma((width_n - 1,)),
                dma((width_n - 1,)),
            ],
            compiler_params=pltpu.CompilerParams(collective_id=0, has_side_effects=True),
            name="scan_norm",
        )(leak_rate[0], signal_in[0], norm_gain[None])
        return out[None]

    return jax.shard_map(
        per_device,
        mesh=mesh,
        in_specs=(P(None, "seq", "width"), P(None, "seq", "width"), P("width")),
        out_specs=P(None, "seq", "width"),
        check_vma=False,
    )
```

time: 176 us -> 25.4 us (0.14)
  local copies, waits for them, and re-layouts: 100 us -> 1.87 us
  other arithmetic: 31.5 us -> 0 us
  Pallas kernels: 0 us -> 23.4 us
  blocking collectives: 19.8 us -> 0 us
  starting transfers between devices: 14.2 us -> 0 us
  waiting for transfers between devices: 6.32 us -> 0 us
  between operations: 2.08 us -> 0.01 us
    slice x154 -> x0, local copies, waits for them, and re-layouts: 39.4 us -> none  [the longest x76 23.8 us: per_device(): lax.associative_scan(join_pair, (keep, push), axis=1, reverse=True)]
    pad x80 -> x0, local copies, waits for them, and re-layouts: 35 us -> none  [the longest x40 21.6 us: per_device(): lax.associative_scan(join_pair, (keep, push), axis=1, reverse=True)]
    pallas_call x0 -> x1, Pallas kernels: none -> 23.4 us  [per_device(): pl.pallas_call(functools.partial(kernel, length, channels, seq_sizes, wid...]
    all_to_all x1 -> x0, blocking collectives: 19.8 us -> none  [copy_for_each(): lax.all_to_all(jnp.broadcast_to(x[None], (length, *x.shape)), axis, 0, 0,...]
    all_to_all x2 -> x0, starting transfers between devices: 14.2 us -> none  [copy_for_each(): lax.all_to_all(jnp.broadcast_to(x[None], (length, *x.shape)), axis, 0, 0,...]
    rev x2 -> x0, local copies, waits for them, and re-layouts: 14.1 us -> none  [per_device(): lax.associative_scan(join_pair, (keep, push), axis=1, reverse=True)]
    mul x47 -> x0, other arithmetic: 8.46 us -> none  [the longest x44 7.33 us: join_pair(): return (earlier[0] * later[0], later[0] * earlier[1] + later[1])]
    add x40 -> x0, other arithmetic: 7.81 us -> none  [the longest x21 5.9 us: per_device(): lax.associative_scan(join_pair, (keep, push), axis=1, reverse=True)]
  transfers between devices with their start and end apart: 2 -> 0, of which waited for: 1 -> 0; matrix products, arithmetic and copies ran while one was open for 29% -> 0% of each run, Pallas kernels for 0% -> 0%
where the time goes in v1:
time: 25.4 us; the launch traced here: 25.3 us
  Pallas kernels  23.4 us (92%)
  local copies, waits for them, and re-layouts  1.87 us (7%)
    pallas_call x1, Pallas kernels, per_device(): pl.pallas_call(functools.partial(kernel, length, channels, seq_sizes, wid...  23.4 us
    unnamed x1, local copies, waits for them, and re-layouts  1.87 us

profile of v1, /device:TPU:1, one launch (start us, length us, event | category | flops | bytes accessed | tf_op | source)
XLA Modules:
  0.0 25.3 jit_solution(7827451289757518307)
XLA Ops:
  0.0 23.4 %scan_norm.1 = bf16[2048,128]{1,0:T(8,128)(2,1)} custom-call(f32[2048,128]{1,0:T(8,128)} %bitcast.5, bf16[2048,128]{1,0:T(8,128)(2,1)} %bitcast.6, f32[1,128]{1,0:T(1,128)} %bitcast.7), custom_call_target="tpu_custom_call" | custom-call | tf_op jit(solution)/shard_map/scan_norm/pallas_call | solution.py:219
  23.4 1.9 %copy.5 = bf16[1,2048,128]{2,1,0:T(8,128)(2,1)} copy(bf16[1,2048,128]{2,1,0:T(8,128)(2,1)} %bitcast.4) | data formatting | bytes 1048576

commit v2 on v1

v2 whole, which is shorter than its diff:
```python
import functools
import math

import jax
import jax.numpy as jnp
from jax import lax
from jax.experimental import pallas as pl
from jax.experimental.pallas import tpu as pltpu
from jax.sharding import PartitionSpec as P

MESH = pl.DeviceIdType.MESH
ROWS = 128
NT = (((1,), (1,)), ((), ()))


def ring_order(sizes):
    offsets = [()]
    for n in sizes:
        offsets = [o + (d,) for o in offsets for d in range(n)]
    far = lambda o: sum(min(d, n - d) for d, n in zip(o, sizes))
    return sorted((o for o in offsets if any(o)), key=lambda o: -far(o))


def split(x):
    high = x.astype(jnp.bfloat16)
    return high, (x - high.astype(jnp.float32)).astype(jnp.bfloat16)


def kernel(
    length, channels, seq_sizes, width_sizes,
    leak_hbm, signal_hbm, gain_hbm, states, scale_ref,
    leak, signal, gain, through, grow_f, grow_b, decay, grow,
    carried_f, decayed_f, carried_b, decayed_b,
    own_carry, got_carry, own_power, got_power,
    in_sem, gain_sem, carry_send, carry_recv, power_send, power_recv,
):
    f32 = jnp.float32
    seq_n, width_n = seq_sizes[0] * seq_sizes[1], width_sizes[0] * width_sizes[1]
    seq, width = lax.axis_index("seq"), lax.axis_index("width")
    blocks = leak.shape[0] // ROWS

    def partner(here, sizes, offset):
        major = lax.rem(here // sizes[1] + offset[0], sizes[0])
        minor = lax.rem(lax.rem(here, sizes[1]) + offset[1], sizes[1])
        return major * sizes[1] + minor

    seq_partners = [partner(seq, seq_sizes, o) for o in ring_order(seq_sizes)]
    width_partners = [partner(width, width_sizes, o) for o in ring_order(width_sizes)]

    with jax.named_scope("greet"):
        barrier = pltpu.get_barrier_semaphore()
        for other in seq_partners:
            pl.semaphore_signal(barrier, inc=1, device_id={"seq": other}, device_id_type=MESH)
        for other in width_partners:
            pl.semaphore_signal(barrier, inc=1, device_id={"width": other}, device_id_type=MESH)
        parts = in_sem.shape[1]
        part = leak.shape[0] // parts
        loads = []
        for k in range(parts):
            rows = pl.ds(k * part, part)
            loads.append((
                pltpu.make_async_copy(leak_hbm.at[rows], leak.at[rows], in_sem.at[0, k]),
                pltpu.make_async_copy(signal_hbm.at[rows], signal.at[rows], in_sem.at[1, k]),
            ))
            for load in loads[-1]:
                load.start()
        gain_load = pltpu.make_async_copy(gain_hbm, gain, gain_sem)
        gain_load.start()


    row = lax.broadcasted_iota(jnp.int32, (ROWS, ROWS), 0)
    col = lax.broadcasted_iota(jnp.int32, (ROWS, ROWS), 1)
    upto = jnp.where(col <= row, 1.0, 0.0).astype(jnp.bfloat16)
    upto = jnp.concatenate([upto, upto], axis=1)

    unit = math.log2(math.e) / length
    ends, sums_f, sums_b = [], [], []
    with jax.named_scope("local"):
        for pair in range(blocks // 2):
            if (pair * 2 * ROWS) % part == 0:
                for load in loads[pair * 2 * ROWS // part]:
                    load.wait()
            two = [pl.ds((2 * pair + side) * ROWS, ROWS) for side in (0, 1)]
            pieces = [split(leak[rows]) for rows in two]
            summed = jnp.dot(
                upto,
                jnp.concatenate(
                    [jnp.concatenate([p[k] for p in pieces], axis=1) for k in (0, 1)], axis=0
                ),
                preferred_element_type=f32,
            )
            for side in (0, 1):
                rows = two[side]
                inside = summed[:, side * ROWS : (side + 1) * ROWS]
                wide = signal[rows].astype(f32)
                up_f = jnp.exp2(inside * unit)
                up_b = jnp.exp2((leak[rows] - inside) * unit)
                through[rows], grow_f[rows], grow_b[rows] = inside, up_f, up_b
                ends.append(jnp.exp2(inside[ROWS - 1 :] * -unit))
                sums_f.append(ends[-1] * jnp.sum(wide * up_f, axis=0, keepdims=True))
                sums_b.append(jnp.sum(wide * up_b, axis=0, keepdims=True))

    with jax.named_scope("ends"):
        at, product = jnp.zeros_like(ends[0]), jnp.ones_like(ends[0])
        for b in range(blocks):
            carried_f[b : b + 1] = at
            decayed_f[b : b + 1] = product
            at, product = at * ends[b] + sums_f[b], product * ends[b]
        own_carry[0:1] = product
        own_carry[1:2] = at
        at, product = jnp.zeros_like(ends[0]), jnp.ones_like(ends[0])
        for b in reversed(range(blocks)):
            at, product = at * ends[b] + sums_b[b], product * ends[b]
            carried_b[b : b + 1] = at
            decayed_b[b : b + 1] = product
        own_carry[2:3] = at
        got_carry[seq] = own_carry[...]


    with jax.named_scope("barrier"):
        pl.semaphore_wait(barrier, seq_n + width_n - 2)


    sends = []
    with jax.named_scope("send_carry"):
        for k, other in enumerate(seq_partners):
            sends.append(pltpu.make_async_remote_copy(
                src_ref=own_carry, dst_ref=got_carry.at[seq],
                send_sem=carry_send.at[k], recv_sem=carry_recv.at[k],
                device_id={"seq": other}, device_id_type=MESH,
            ))
            sends[-1].start()

    with jax.named_scope("inner"):
        for b in range(blocks):
            rows = pl.ds(b * ROWS, ROWS)
            push = signal[rows]
            wide, inside = push.astype(f32), through[rows]
            extra_f = (wide * (grow_f[rows] - 1.0)).astype(jnp.bfloat16)
            extra_b = (wide * (grow_b[rows] - 1.0)).astype(jnp.bfloat16)
            both = jnp.dot(
                upto,
                jnp.concatenate(
                    [
                        jnp.concatenate([push, push], axis=1),
                        jnp.concatenate([extra_f, extra_b], axis=1),
                    ],
                    axis=0,
                ),
                preferred_element_type=f32,
            )
            down, up = jnp.exp2(inside * -unit), jnp.exp2((inside - leak[rows]) * unit)
            decay[rows], grow[rows] = down, up
            states[rows] = down * both[:, :ROWS] + (wide - up * both[:, ROWS:])

    with jax.named_scope("wait_carry"):
        for send in sends:
            send.wait_recv()

    with jax.named_scope("enter"):
        into_f, into_b = jnp.zeros_like(ends[0]), jnp.zeros_like(ends[0])
        for j in range(seq_n):
            into_f = jnp.where(j < seq, into_f * got_carry[j, 0:1] + got_carry[j, 1:2], into_f)
            i = seq_n - 1 - j
            into_b = jnp.where(i > seq, into_b * got_carry[i, 0:1] + got_carry[i, 2:3], into_b)
        carried_f[...] = carried_f[...] + decayed_f[...] * into_f
        carried_b[...] = carried_b[...] + decayed_b[...] * into_b


    with jax.named_scope("power"):
        ones = jnp.ones((8, 2 * ROWS), jnp.bfloat16)
        for pair in range(blocks // 2):
            squares = []
            for b in (2 * pair, 2 * pair + 1):
                rows = pl.ds(b * ROWS, ROWS)
                value = (
                    states[rows]
                    + decay[rows] * carried_f[b : b + 1]
                    + grow[rows] * carried_b[b : b + 1]
                )
                states[rows] = value
                squares.append(jnp.concatenate(split(value * value), axis=1))
            power = lax.dot_general(
                ones, jnp.concatenate(squares, axis=0), NT, preferred_element_type=f32
            )
            own_power[2 * pair : 2 * pair + 1] = power[0:1, :ROWS]
            own_power[2 * pair + 1 : 2 * pair + 2] = power[0:1, ROWS:]
        got_power[width] = own_power[...]


    with jax.named_scope("send_power"):
        for k, other in enumerate(width_partners):
            send = pltpu.make_async_remote_copy(
                src_ref=own_power, dst_ref=got_power.at[width],
                send_sem=power_send.at[k], recv_sem=power_recv.at[k],
                device_id={"width": other}, device_id_type=MESH,
            )
            send.start()
            sends.append(send)


    with jax.named_scope("gain"):
        gain_load.wait()
        by = gain[...] * length**-0.5
        for b in range(blocks):
            rows = pl.ds(b * ROWS, ROWS)
            states[rows] = states[rows] * by


    with jax.named_scope("wait_power"):
        for send in sends[seq_n - 1 :]:
            send.wait_recv()


    with jax.named_scope("total"):
        total = got_power[0]
        for j in range(1, width_n):
            total = total + got_power[j]
        scale_ref[...] = lax.rsqrt(total * (1.0 / (channels * length)) + 1e-06)

    with jax.named_scope("drain"):
        for send in sends:
            send.wait_send()


def finish(states, scale_ref, out_hbm, out, out_sem):
    blocks, lanes = scale_ref.shape
    parts = out_sem.shape[0]
    part = out.shape[0] // parts
    zeros = jnp.zeros((lanes - blocks, lanes), jnp.float32)
    scale = jnp.concatenate([scale_ref[...], zeros], axis=0).T
    stores = []
    for b in range(blocks):
        rows = pl.ds(b * ROWS, ROWS)
        out[rows] = (states[rows] * scale[:, b : b + 1]).astype(out.dtype)
        if (b + 1) * ROWS % part == 0:
            k = (b + 1) * ROWS // part - 1
            rows = pl.ds(k * part, part)
            stores.append(pltpu.make_async_copy(out.at[rows], out_hbm.at[rows], out_sem.at[k]))
            stores[-1].start()
    for store in stores:
        store.wait()


def solution(mesh):
    sizes = dict(mesh.shape)
    seq_n, width_n = sizes["seq"], sizes["width"]
    seq_sizes, width_sizes = (4, seq_n // 4), (width_n // 2, 2)

    def per_device(leak_rate, signal_in, norm_gain):
        _, rows, lanes = leak_rate.shape
        length, channels = rows * seq_n, lanes * width_n
        blocks = rows // ROWS
        f32 = jnp.float32
        vmem, dma = pltpu.VMEM, pltpu.SemaphoreType.DMA
        here = pl.BlockSpec(memory_space=pltpu.VMEM)
        there = pl.BlockSpec(memory_space=pl.ANY)
        states, scale = pl.pallas_call(
            functools.partial(kernel, length, channels, seq_sizes, width_sizes),
            out_shape=[pltpu.VMEM((rows, lanes), f32), pltpu.VMEM((blocks, lanes), f32)],
            in_specs=[there] * 3,
            out_specs=[here, here],
            scratch_shapes=[
                vmem((rows, lanes), f32),
                vmem((rows, lanes), jnp.bfloat16),
                vmem((1, lanes), f32),
                *[vmem((rows, lanes), f32)] * 5,
                *[vmem((blocks, lanes), f32)] * 4,
                vmem((3, lanes), f32),
                vmem((seq_n, 3, lanes), f32),
                vmem((blocks, lanes), f32),
                vmem((width_n, blocks, lanes), f32),
                dma((2, 4)),
                dma,
                dma((seq_n - 1,)),
                dma((seq_n - 1,)),
                dma((width_n - 1,)),
                dma((width_n - 1,)),
            ],
            compiler_params=pltpu.CompilerParams(collective_id=0, has_side_effects=True),
            name="scan_norm",
        )(leak_rate[0], signal_in[0], norm_gain[None])
        out = pl.pallas_call(
            finish,
            out_shape=jax.ShapeDtypeStruct((rows, lanes), jnp.bfloat16),
            in_specs=[here, here],
            out_specs=there,
            scratch_shapes=[vmem((rows, lanes), jnp.bfloat16), dma((4,))],
            compiler_params=pltpu.CompilerParams(vmem_limit_bytes=8 << 20),
            name="finish",
        )(states, scale)
        return out[None]

    return jax.shard_map(
        per_device,
        mesh=mesh,
        in_specs=(P(None, "seq", "width"), P(None, "seq", "width"), P("width")),
        out_specs=P(None, "seq", "width"),
        check_vma=False,
    )
```

time: 25.4 us -> 22 us (0.87)
  local copies, waits for them, and re-layouts: 1.87 us -> 0 us
  Pallas kernels: 23.4 us -> 21.9 us
    pallas_call x1, Pallas kernels: 23.4 us -> 20.8 us  [per_device(): pl.pallas_call(functools.partial(kernel, length, channels, seq_sizes, wid...]
    unnamed x1 -> x0, local copies, waits for them, and re-layouts: 1.87 us -> none
    pallas_call x0 -> x1, Pallas kernels: none -> 1.16 us  [per_device(): pl.pallas_call(finish, out_shape=jax.ShapeDtypeStruct((rows, lanes), jnp....]
where the time goes in v2:
time: 22 us; the launch traced here: 21.9 us
  Pallas kernels  21.9 us (100%)
    pallas_call x1, Pallas kernels, per_device(): pl.pallas_call(functools.partial(kernel, length, channels, seq_sizes, wid...  20.8 us
    pallas_call x1, Pallas kernels, per_device(): pl.pallas_call(finish, out_shape=jax.ShapeDtypeStruct((rows, lanes), jnp....  1.16 us

profile of v2, /device:TPU:1, one launch (start us, length us, event | category | flops | bytes accessed | tf_op | source)
XLA Modules:
  0.0 21.9 jit_solution(13531711256518880734)
XLA Ops:
  0.0 20.8 %scan_norm.1 = (f32[2048,128]{1,0:T(8,128)S(1)}, f32[16,128]{1,0:T(8,128)S(1)}) custom-call(f32[2048,128]{1,0:T(8,128)} %bitcast.4, bf16[2048,128]{1,0:T(8,128)(2,1)} %bitcast.5, f32[1,128]{1,0:T(1,128)} %bitcast.6), custom_call_target="tpu_custom_call" | custom-call | tf_op jit(solution)/shard_map/scan_norm/pallas_call | solution.py:258
  20.8 1.2 %finish.1 = bf16[2048,128]{1,0:T(8,128)(2,1)} custom-call(f32[2048,128]{1,0:T(8,128)S(1)} %get-tuple-element.7.states, f32[16,128]{1,0:T(8,128)S(1)} %get-tuple-element.8.scale_ref), custom_call_target="tpu_custom_call" | custom-call | tf_op jit(solution)/shard_map/finish/pallas_call | solution.py:283
